TPU v7x, 128 devices: a whole 4x4x4 slice. The times are simulated.
128 devices in a mesh: grp: 2 (over core), seq: 32 (over y, x_lo, z), tp: 2 (over x_hi).
Axes of the slice: x: 4 (x_hi: 2, x_lo: 2; x = x_hi * 2 + x_lo), y: 4, z: 4, core: 2. Of those that a mesh axis runs over, the one named last changes fastest.
Arguments:
- prompt_states: bfloat16 [2, 16384, 4096], P(None, ('grp', 'seq'), 'tp'), may hold values from -40 to 40
- q_weight: bfloat16 [4096, 16, 128], P(None, 'tp'), may hold values from -0.09375 to 0.09375
- kv_weight: bfloat16 [4096, 2, 4, 128], P(None, None, 'tp'), may hold values from -0.09375 to 0.09375
- lengths: int32 [2], replicated, may hold values from 4096 to 16384, as said below
- sink_positions: int32 [2, 4], replicated, may hold values from 0 to 2047
Outputs:
- attended: bfloat16 [2, 16384, 2048], P(None, ('grp', 'seq'), 'tp')
- kv_cache: bfloat16 [2, 4, 2, 32, 256, 256], P(None, ('tp', 'grp'), None, 'seq')
Inputs may be any that keep to these rules, and one draw needn't show every extreme that they name: `lengths`: at least one request has length 16384.
All inputs are finite; a program needn't handle non-finite values.
Results may differ from a plain program's by a relative error of at most 0.0065.
Values may be sent and summed in bfloat16 or wider, within the bound.
A program may use at most 256 MiB of HBM per device.

v0:
```python
import math

import jax
import jax.numpy as jnp
from jax import lax
from jax.experimental import pallas as pl
from jax.experimental.pallas import tpu as pltpu
from jax.sharding import PartitionSpec as P

WINDOW = 4096
ROPE_BASE = 10000.0
NEG_FILL = -1e30
FAR = 1 << 30
MESH = pl.DeviceIdType.MESH
CHUNKS = 4
VMEM_BYTES = 60 * 2**20


def place():
    core, seq, tp = lax.axis_index("grp"), lax.axis_index("seq"), lax.axis_index("tp")
    return core, seq // 8, lax.rem(seq // 4, 2), lax.rem(seq, 4), tp


def at(core, y, x, z, tp):
    return (core, y * 8 + x * 4 + z, tp)


def next_row(core, y):
    wraps = (y + 1) // 4
    return lax.rem(core + wraps, 2), lax.rem(y + 1, 4)


def previous_row(core, y):
    wraps = (4 - y) // 4
    return lax.rem(core + wraps, 2), lax.rem(y + 3, 4)


def remote(src, dst, send_sem, recv_sem, target):
    return pltpu.make_async_remote_copy(
        src_ref=src,
        dst_ref=dst,
        send_sem=send_sem,
        recv_sem=recv_sem,
        device_id=target,
        device_id_type=MESH,
    )


def turned(block, cosine, sine):
    return block * cosine + pltpu.roll(block, 64, 1) * sine


def gather_kernel(
    lens, x_hbm, wq_hbm, wkv_hbm, cos_ref, sin_ref, hot_ref,
    q_out, kv_out, sink_out, cache_out,
    x_own, x_far, wq, wkv, acc_q, acc_kv, q_stage, kv_stage, cache_stage, group_kv, sink_stage,
    x_send, x_recv, load_sem, kv_send, kv_recv, kv_keep, q_send, q_recv, q_keep,
    a_send, a_recv, b_send, b_recv, aa_send, aa_recv, bb_send, bb_recv,
    c_send, c_recv, c_keep, s_send, s_recv, s_keep,
):
    core, y, x, z, tp = place()
    up, down = next_row(core, y), previous_row(core, y)
    ahead, behind = at(*up, x, z, tp), at(*down, x, z, tp)
    partner = at(core, y, x, z, 1 - tp)
    twin = at(1 - core, y, x, z, tp)
    side_core = core * (1 - x) + up[0] * x
    side_y = y * (1 - x) + up[1] * x
    side = at(side_core, side_y, 1 - x, z, tp)
    feed_core = core * x + down[0] * (1 - x)
    feed_y = y * x + down[1] * (1 - x)
    feed = at(feed_core, feed_y, 1 - x, z, tp)
    first_row = (core + y) == 0
    row = core * 4 + y
    peers = [at(core, y, x, lax.rem(z + d, 4), tp) for d in (1, 2, 3)]

    barrier = pltpu.get_barrier_semaphore()
    for other in [partner, twin, ahead, behind, side, feed, *peers]:
        pl.semaphore_signal(barrier, inc=1, device_id=other, device_id_type=MESH)

    def sink_target(n):
        slot = lax.rem(row * 2 + x + n, 16)
        return at(slot // 8, lax.rem(slot // 2, 4), lax.rem(slot, 2), z, tp)

    @pl.when(first_row)
    def _():
        for n in range(1, 16):
            pl.semaphore_signal(barrier, inc=1, device_id=sink_target(n), device_id_type=MESH)
        pl.semaphore_wait(barrier, 24)

    @pl.when(jnp.logical_not(first_row))
    def _():
        for x_home in (0, 1):
            pl.semaphore_signal(
                barrier, inc=1, device_id=at(0, 0, x_home, z, tp), device_id_type=MESH
            )
        pl.semaphore_wait(barrier, 11)

    size = 256 // CHUNKS
    spans = [pl.ds(c * size, size) for c in range(CHUNKS)]
    x_copies = [
        remote(x_hbm.at[:, s], x_far.at[:, s], x_send.at[c], x_recv.at[c], partner)
        for c, s in enumerate(spans)
    ]
    for copy in x_copies:
        copy.start()
    loads = [
        pltpu.make_async_copy(x_hbm, x_own, load_sem.at[0]),
        pltpu.make_async_copy(wkv_hbm, wkv, load_sem.at[1]),
        pltpu.make_async_copy(wq_hbm, wq, load_sem.at[2]),
    ]
    for copy in loads:
        copy.start()
    for copy in loads:
        copy.wait()
    own_rows = pl.ds(pl.multiple_of(tp * 2048, 2048), 2048)
    far_rows = pl.ds(pl.multiple_of((1 - tp) * 2048, 2048), 2048)

    def columns(n):
        return pl.ds(pl.multiple_of(n * 256, 256), 256)

    @pl.loop(0, 2)
    def _(n):
        acc_kv[:, :, columns(n)] = jnp.dot(
            x_own[...].reshape(512, 2048),
            wkv[own_rows, columns(n)],
            preferred_element_type=jnp.float32,
        ).reshape(2, 256, 256)

    @pl.loop(0, 4)
    def _(n):
        acc_q[:, :, columns(n)] = jnp.dot(
            x_own[...].reshape(512, 2048),
            wq[own_rows, columns(n)],
            preferred_element_type=jnp.float32,
        ).reshape(2, 256, 256)

    slab_start = (core * 32 + y * 8 + x * 4 + z) * 256
    pending = []
    kv_copies, q_copies, keeps, a_copies, b_copies, aa_copies, bb_copies = [], [], [], [], [], [], []

    def pass_on(c):
        s = spans[c]
        a_copies[c].wait_recv()
        aa = remote(
            kv_out.at[8:12, s], kv_out.at[0:4, s], aa_send.at[c], aa_recv.at[c], ahead
        )
        aa.start()
        aa_copies.append(aa)
        b_copies[c].wait_recv()
        bb = remote(
            kv_out.at[12:16, s], kv_out.at[4:8, s], bb_send.at[c], bb_recv.at[c], ahead
        )
        bb.start()
        bb_copies.append(bb)

    for c in range(CHUNKS):
        s = spans[c]
        x_copies[c].wait_recv()
        cosine, sine = cos_ref[s, :], sin_ref[s, :]

        @pl.loop(0, 2)
        def _(n):
            total = jnp.dot(
                x_far[:, s].reshape(2 * size, 2048),
                wkv[far_rows, columns(n)],
                preferred_element_type=jnp.float32,
            )
            for r in range(2):
                block = total[r * size:(r + 1) * size] + acc_kv[r, s, columns(n)]
                keys = turned(block[:, :128], cosine, sine).astype(jnp.bfloat16)
                both = jnp.concatenate([keys, block[:, 128:].astype(jnp.bfloat16)], axis=1)
                kv_stage[r * 2 + n, s, :] = both
                position = (
                    slab_start + c * size + lax.broadcasted_iota(jnp.int32, (size, 256), 0)
                )
                cache_stage[r, n, s, :] = jnp.where(
                    position < lens[r], both.astype(jnp.float32), 0.0
                ).astype(jnp.bfloat16)

        for d in (1, 2, 3):
            target = lax.rem(z + d, 4)
            copy = remote(
                kv_stage.at[target, s], kv_out.at[16 + z, s],
                kv_send.at[c, d - 1], kv_recv.at[c, d - 1], peers[d - 1],
            )
            copy.start()
            kv_copies.append(copy)
        keep = pltpu.make_async_copy(kv_stage.at[z, s], kv_out.at[16 + z, s], kv_keep.at[c])
        keep.start()

        @pl.loop(0, 4)
        def _(n):
            total = jnp.dot(
                x_far[:, s].reshape(2 * size, 2048),
                wq[far_rows, columns(n)],
                preferred_element_type=jnp.float32,
            )
            for r in range(2):
                block = total[r * size:(r + 1) * size] + acc_q[r, s, columns(n)]
                for k in range(2):
                    head = turned(block[:, k * 128:(k + 1) * 128], cosine, sine)
                    q_stage[r * 2 + n // 2, lax.rem(n, 2) * 2 + k, s, :] = head.astype(
                        jnp.bfloat16
                    )

        for d in (1, 2, 3):
            target = lax.rem(z + d, 4)
            copy = remote(
                q_stage.at[target, :, s], q_out.at[z, :, s],
                q_send.at[c, d - 1], q_recv.at[c, d - 1], peers[d - 1],
            )
            copy.start()
            q_copies.append(copy)
        q_own = pltpu.make_async_copy(q_stage.at[z, :, s], q_out.at[z, :, s], q_keep.at[c])
        q_own.start()
        keeps.append(q_own)

        keep.wait()
        for d in range(3):
            kv_copies[c * 3 + d].wait_recv()
        a = remote(kv_out.at[16:20, s], kv_out.at[8:12, s], a_send.at[c], a_recv.at[c], ahead)
        b = remote(kv_out.at[16:20, s], kv_out.at[12:16, s], b_send.at[c], b_recv.at[c], side)
        a.start()
        b.start()
        a_copies.append(a)
        b_copies.append(b)
        if c >= 1:
            pass_on(c - 1)

    cache_copy = remote(
        cache_stage.at[:, 1 - core], cache_out.at[:, core], c_send.at[0], c_recv.at[0], twin
    )
    cache_copy.start()
    cache_keep = pltpu.make_async_copy(
        cache_stage.at[:, core], cache_out.at[:, core], c_keep.at[0]
    )
    cache_keep.start()

    sink_sends = [
        remote(
            sink_stage, sink_out.at[x], s_send.at[n - 1], s_recv.at[x], sink_target(n)
        )
        for n in range(1, 16)
    ]
    sink_keep = pltpu.make_async_copy(sink_stage, sink_out.at[x], s_keep.at[0])

    @pl.when(first_row)
    def _():
        load = pltpu.make_async_copy(kv_out.at[16:20], group_kv, load_sem.at[0])
        load.start()
        load.wait()
        sink_stage[...] = jnp.dot(
            hot_ref[...], group_kv[...].reshape(1024, 256), preferred_element_type=jnp.float32
        ).astype(jnp.bfloat16)
        for copy in sink_sends:
            copy.start()
        sink_keep.start()

    pass_on(CHUNKS - 1)

    @pl.when(first_row)
    def _():
        sink_keep.wait()
        for copy in sink_sends:
            copy.wait_send()
        remote(sink_stage, sink_out.at[1 - x], s_send.at[0], s_recv.at[1 - x], partner).wait_recv()

    @pl.when(jnp.logical_not(first_row))
    def _():
        for home in (0, 1):
            remote(
                sink_stage, sink_out.at[home], s_send.at[0], s_recv.at[home], partner
            ).wait_recv()

    for copy in keeps:
        copy.wait()
    cache_keep.wait()
    cache_copy.wait()
    for copy in aa_copies + bb_copies:
        copy.wait()
    for copy in q_copies:
        copy.wait()
    for copy in kv_copies + a_copies + b_copies + x_copies:
        copy.wait_send()


SCALE = math.log2(math.e) / math.sqrt(128.0)


def attend_kernel(
    lens, sink_pos, q_ref, kv_ref, sink_ref, out_ref,
    values, peak, total, stage, send_sem, recv_sem, keep_sem,
):
    core, y, x, z, tp = place()
    group = (core * 4 + y) * 2 + x
    peers = [at(core, y, x, lax.rem(z + d, 4), tp) for d in (1, 2, 3)]
    barrier = pltpu.get_barrier_semaphore()
    for other in peers:
        pl.semaphore_signal(barrier, inc=1, device_id=other, device_id_type=MESH)
    pl.semaphore_wait(barrier, 3)

    values[:, :, :128] = kv_ref[:, :, 128:]
    values[:, :, 128:] = jnp.ones((20, 256, 128), jnp.bfloat16)
    request = z // 2
    length = lens[request]
    sink_kv = (sink_ref[0].astype(jnp.float32) + sink_ref[1].astype(jnp.float32)).astype(
        jnp.bfloat16
    )
    pad = jnp.zeros((112, 128), jnp.bfloat16)
    sink_keys = jnp.concatenate([sink_kv[:, :128], pad], axis=0)
    sink_values = jnp.concatenate(
        [
            jnp.concatenate([sink_kv[:, 128:], pad], axis=0),
            jnp.ones((128, 128), jnp.bfloat16),
        ],
        axis=1,
    )

    def fold(queries, keys, vals, visible):
        scores = lax.dot_general(
            queries, keys, (((1,), (1,)), ((), ())), preferred_element_type=jnp.float32
        )
        if visible is not None:
            width = scores.shape[1]
            scores = jnp.where(
                visible[None], scores.reshape(4, 256, width), NEG_FILL
            ).reshape(1024, width)
        old = peak[...]
        new = jnp.maximum(old, jnp.max(scores, axis=1, keepdims=True))
        peak[...] = new
        shift = new[:, :1] * SCALE
        weights = jnp.exp2(scores * SCALE - shift).astype(jnp.bfloat16)
        factor = jnp.exp2((old - new) * SCALE)
        gained = jnp.dot(weights, vals, preferred_element_type=jnp.float32)
        total[...] = total[...] * jnp.concatenate([factor, factor], axis=1) + gained

    def block_mask(first_query, first_key):
        query = first_query + lax.broadcasted_iota(jnp.int32, (256, 256), 0)
        key = first_key + lax.broadcasted_iota(jnp.int32, (256, 256), 1)
        return (query - key >= 0) & (query - key < WINDOW)

    for turn in range(4):
        j = lax.rem(z + 1 + turn, 4)
        queries = q_ref[j].reshape(1024, 128)
        peak[...] = jnp.full((1024, 128), NEG_FILL, jnp.float32)
        total[...] = jnp.zeros((1024, 256), jnp.float32)
        first_query = (16 + j) * 256
        edge_count = jnp.where(group >= 4, 5, j + 1)

        def edge(t, carry):
            slab = jnp.where(t <= j, 16 + j - t, t - 1)
            fold(
                queries, kv_ref[slab, :, :128], values[slab],
                block_mask(first_query, slab * 256),
            )
            return carry

        lax.fori_loop(0, edge_count, edge, 0)

        def middle(k, carry):
            first = 12 - 4 * k
            fold(
                queries,
                kv_ref[pl.ds(first, 4), :, :128].reshape(1024, 128),
                values[pl.ds(first, 4)].reshape(1024, 256),
                None,
            )
            return carry

        lax.fori_loop(0, jnp.minimum(group, 3), middle, 0)
        true_first = (group * 4 + j) * 256
        query_pos = true_first + lax.broadcasted_iota(jnp.int32, (256, 128), 0)
        fold(queries, sink_keys, sink_values, query_pos - sink_pos[...] >= WINDOW)
        mixed = total[:, :128] / total[:, 128:]
        for h in range(4):
            part = mixed[h * 256:(h + 1) * 256]
            stage[turn, :, h * 128:(h + 1) * 128] = jnp.where(
                query_pos < length, part, 0.0
            ).astype(jnp.bfloat16)
        home = out_ref.at[
            request, :, pl.ds(pl.multiple_of(lax.rem(z, 2) * 512, 512), 512)
        ]
        if turn < 3:
            remote(
                stage.at[turn], home, send_sem.at[turn], recv_sem.at[turn], peers[turn]
            ).start()
        else:
            keep = pltpu.make_async_copy(stage.at[3], home, keep_sem.at[0])
            keep.start()
    keep.wait()
    for turn in range(3):
        source = lax.rem(z + 3 - turn, 4)
        landed = out_ref.at[
            source // 2, :, pl.ds(pl.multiple_of(lax.rem(source, 2) * 512, 512), 512)
        ]
        remote(
            stage.at[turn], landed, send_sem.at[turn], recv_sem.at[turn], peers[turn]
        ).wait()


def dma(*shape):
    return pltpu.SemaphoreType.DMA(shape)


def per_device(prompt_states, q_weight, kv_weight, lengths, sink_positions):
    bf16 = jnp.bfloat16
    core, y, x, z, tp = place()
    group = (core * 4 + y) * 2 + x
    wq = q_weight.reshape(4096, 1024)
    wkv = jnp.transpose(kv_weight, (0, 2, 1, 3)).reshape(4096, 512)
    positions = (group * 4 + z) * 256 + jnp.arange(256, dtype=jnp.int32)
    ladder = jnp.arange(64, dtype=jnp.float32) * (2.0 / 128)
    inv_freq = jnp.exp(-math.log(ROPE_BASE) * ladder)
    angles = positions.astype(jnp.float32)[:, None] * inv_freq[None, :]
    cosine, sine = jnp.cos(angles), jnp.sin(angles)
    cos_table = jnp.concatenate([cosine, cosine], axis=1)
    sin_table = jnp.concatenate([-sine, sine], axis=1)
    sinks = jnp.where(z < 2, sink_positions[0], sink_positions[1])
    group_pos = group * 1024 + jnp.arange(1024, dtype=jnp.int32)
    hot = (sinks[:, None] == group_pos[None, :]).astype(bf16)
    hot = jnp.pad(hot, ((0, 12), (0, 0)))
    earlier = jnp.arange(4)[None, :] < jnp.arange(4)[:, None]
    repeated = jnp.any((sinks[:, None] == sinks[None, :]) & earlier, axis=1)
    sink_row = jnp.pad(jnp.where(repeated, FAR, sinks), (0, 124), constant_values=FAR)[None]

    anyspace = pl.BlockSpec(memory_space=pl.ANY)
    vmem = pl.BlockSpec(memory_space=pltpu.VMEM)
    smem = pl.BlockSpec(memory_space=pltpu.SMEM)
    shape = jax.ShapeDtypeStruct
    q_all, kv_all, sink_kv, cache = pl.pallas_call(
        gather_kernel,
        out_shape=(
            shape((4, 4, 256, 128), bf16),
            shape((20, 256, 256), bf16),
            shape((2, 16, 256), bf16),
            shape((2, 2, 256, 256), bf16),
        ),
        in_specs=[smem, anyspace, anyspace, anyspace, vmem, vmem, vmem],
        out_specs=(anyspace, anyspace, anyspace, anyspace),
        scratch_shapes=[
            pltpu.VMEM((2, 256, 2048), bf16),
            pltpu.VMEM((2, 256, 2048), bf16),
            pltpu.VMEM((4096, 1024), bf16),
            pltpu.VMEM((4096, 512), bf16),
            pltpu.VMEM((2, 256, 1024), jnp.float32),
            pltpu.VMEM((2, 256, 512), jnp.float32),
            pltpu.VMEM((4, 4, 256, 128), bf16),
            pltpu.VMEM((4, 256, 256), bf16),
            pltpu.VMEM((2, 2, 256, 256), bf16),
            pltpu.VMEM((4, 256, 256), bf16),
            pltpu.VMEM((16, 256), bf16),
            dma(CHUNKS), dma(CHUNKS), dma(3),
            dma(CHUNKS, 3), dma(CHUNKS, 3), dma(CHUNKS),
            dma(CHUNKS, 3), dma(CHUNKS, 3), dma(CHUNKS),
            dma(CHUNKS), dma(CHUNKS), dma(CHUNKS), dma(CHUNKS),
            dma(CHUNKS), dma(CHUNKS), dma(CHUNKS), dma(CHUNKS),
            dma(1), dma(1), dma(1), dma(15), dma(2), dma(1),
        ],
        compiler_params=pltpu.CompilerParams(
            collective_id=0, has_side_effects=True, vmem_limit_bytes=VMEM_BYTES
        ),
    )(lengths, prompt_states, wq, wkv, cos_table, sin_table, hot)
    attended = pl.pallas_call(
        attend_kernel,
        out_shape=shape((2, 256, 1024), bf16),
        in_specs=[smem, vmem, vmem, vmem, vmem],
        out_specs=anyspace,
        scratch_shapes=[
            pltpu.VMEM((20, 256, 256), bf16),
            pltpu.VMEM((1024, 128), jnp.float32),
            pltpu.VMEM((1024, 256), jnp.float32),
            pltpu.VMEM((4, 256, 512), bf16),
            dma(3), dma(3), dma(1),
        ],
        compiler_params=pltpu.CompilerParams(
            collective_id=1, has_side_effects=True, vmem_limit_bytes=VMEM_BYTES
        ),
    )(lengths, sink_row, q_all, kv_all, sink_kv)
    return attended, cache.reshape(2, 1, 2, 1, 256, 256)


def solution(mesh):
    placed = (
        P(None, ("grp", "seq"), "tp"),
        P(None, "tp", None),
        P(None, None, "tp", None),
        P(),
        P(),
    )
    return jax.shard_map(
        per_device,
        mesh=mesh,
        in_specs=placed,
        out_specs=(P(None, ("grp", "seq"), "tp"), P(None, ("tp", "grp"), None, "seq", None, None)),
        check_vma=False,
    )
```

profile of v0, /device:TPU:1, one launch (start us, length us, event | category | flops | bytes accessed | tf_op | source)
XLA Modules:
  0.0 191.6 jit_solution(1649295240035948834)
XLA Ops:
  0.7 0.8 fusion.3
  1.4 0.2 fusion.2
  1.6 0.8 broadcast_select_fusion.1
  2.4 0.5 pad_bitcast_fusion.sink_pos
  2.9 0.1 broadcast_compare_fusion
  3.0 0.6 pad_convert_fusion.hot_ref
  3.6 0.5 fusion
  4.2 0.8 pad_maximum_fusion
  5.0 10.8 %copy.9 = bf16[4096,2,2,128]{3,2,1,0:T(2,128)(2,1)} copy(bf16[4096,2,2,128]{3,1,2,0:T(2,128)(2,1)} %bitcast.16) | data formatting | bytes 8388608 | tf_op jit(solution)/shard_map/transpose | solution.py:410
  15.8 7.2 %reshape.39.wkv_hbm = bf16[4096,512]{1,0:T(8,128)(2,1)} reshape(bf16[4096,2,2,128]{3,2,1,0:T(2,128)(2,1)} %copy.9) | data formatting | bytes 8388608 | tf_op jit(solution)/shard_map/reshape | solution.py:410
  23.0 8.8 %copy.13 = bf16[512,8,8,128]{3,1,2,0:T(8,128)(2,1)} copy(bf16[512,8,8,128]{3,2,1,0:T(8,128)(2,1)} %bitcast.15) | data formatting | bytes 16777216
  31.7 93.2 %shard_map.68 = (bf16[4,4,256,128]{3,2,1,0:T(8,128)(2,1)}, bf16[20,256,256]{2,1,0:T(8,128)(2,1)}, bf16[2,16,256]{2,1,0:T(8,128)(2,1)}, bf16[2,2,256,256]{3,2,1,0:T(8,128)(2,1)}) custom-call(s32[2]{0:T(128)} %lens.3, bf16[2,256,2048]{2,1,0:T(8,128)(2,1)} %x_hbm.1, bf16[4096,1024]{1,0:T(8,128)(2,1)} %bitcast.14, bf16[4096,512]{1,0:T(8,128)(2,1)} %reshape.39.wkv_hbm, ...), custom_call_target="tpu_custom_call" | custom-call | tf_op jit(solution)/shard_map/pallas_call | solution.py:430
  125.0 0.0 copy-start
  125.0 63.6 %shard_map.69 = bf16[2,256,1024]{2,1,0:T(8,128)(2,1)} custom-call(s32[2]{0:T(128)} %lens.3, s32[1,128]{1,0:T(1,128)} %pad_bitcast_fusion.sink_pos, bf16[4,4,256,128]{3,2,1,0:T(8,128)(2,1)} %get-tuple-element.6.q_ref, bf16[20,256,256]{2,1,0:T(8,128)(2,1)} %get-tuple-element.7.kv_ref, bf16[2,16,256]{2,1,0:T(8,128)(2,1)} %get-tuple-element.8.sink_ref), custom_call_target="tpu_custom_call" | custom-call | tf_op jit(solution)/shard_map/pallas_call | solution.py:463
  188.6 2.3 %copy.16 = bf16[2,256,1024]{2,1,0:T(8,128)(2,1)} copy(bf16[2,256,1024]{2,1,0:T(8,128)(2,1)} %shard_map.69) | data formatting | bytes 2097152
  190.8 0.0 copy-done
  190.9 0.8 copy.17
  (3 shorter events, 0.0 us)
Async XLA Ops:
  125.0 65.9 %copy-start = (bf16[2,2,256,256]{3,2,1,0:T(8,128)(2,1)S(1)}, bf16[2,2,256,256]{3,2,1,0:T(8,128)(2,1)}, u32[]{:S(2)}) copy-start(bf16[2,2,256,256]{3,2,1,0:T(8,128)(2,1)} %get-tuple-element.9) | copy-start | bytes 1572868
where the time goes:
time: 192 us
  Pallas kernels  157 us (82%)
  local copies, waits for them, and re-layouts  30.3 us (16%)
  other arithmetic  3.78 us (2%)
    pallas_call x1, Pallas kernels, per_device(): pl.pallas_call(gather_kernel, out_shape=(shape((4, 4, 256, 128), bf16), s...  93.2 us
    pallas_call x1, Pallas kernels, per_device(): pl.pallas_call(attend_kernel, out_shape=shape((2, 256, 1024), bf16), in_s...  63.6 us
    unnamed x5, local copies, waits for them, and re-layouts  11.8 us
    transpose x1, local copies, waits for them, and re-layouts, per_device(): wkv = jnp.transpose(kv_weight, (0, 2, 1, 3)).reshape(4096, 512)  10.8 us
    reshape x1, local copies, waits for them, and re-layouts, per_device(): wkv = jnp.transpose(kv_weight, (0, 2, 1, 3)).reshape(4096, 512)  7.21 us

commit v1 on v0

v1 whole, which is shorter than its diff:
```python
import math

import jax
import jax.numpy as jnp
from jax import lax
from jax.experimental import pallas as pl
from jax.experimental.pallas import tpu as pltpu
from jax.sharding import PartitionSpec as P

WINDOW = 4096
ROPE_BASE = 10000.0
NEG_FILL = -1e30
FAR = 1 << 30
MESH = pl.DeviceIdType.MESH
CHUNKS = 4
VMEM_BYTES = 60 * 2**20


def place():
    core, seq, tp = lax.axis_index("grp"), lax.axis_index("seq"), lax.axis_index("tp")
    return core, seq // 8, lax.rem(seq // 4, 2), lax.rem(seq, 4), tp


def at(core, y, x, z, tp):
    return (core, y * 8 + x * 4 + z, tp)


def next_row(core, y):
    wraps = (y + 1) // 4
    return lax.rem(core + wraps, 2), lax.rem(y + 1, 4)


def previous_row(core, y):
    wraps = (4 - y) // 4
    return lax.rem(core + wraps, 2), lax.rem(y + 3, 4)


def remote(src, dst, send_sem, recv_sem, target):
    return pltpu.make_async_remote_copy(
        src_ref=src,
        dst_ref=dst,
        send_sem=send_sem,
        recv_sem=recv_sem,
        device_id=target,
        device_id_type=MESH,
    )


def turned(block, cosine, sine):
    return block * cosine + pltpu.roll(block, 64, 1) * sine


SCALE = math.log2(math.e) / math.sqrt(128.0)


def layer_kernel(
    lens, x_hbm, wq_hbm, wkv_hbm, cos_ref, sin_ref, hot_ref, sink_pos,
    out_ref, cache_out,
    x_own, x_far, wq_raw, wkv_raw, spread, wq, wkv, acc_q, acc_kv, q_stage, kv_stage, cache_stage,
    q_all, kv_all, sink_all, sink_stage, values, sink_values, peak, total, scores, stage,
    x_send, x_recv, load_sem, kv_send, kv_recv, kv_keep, q_send, q_recv, q_keep,
    a_send, a_recv, b_send, b_recv, aa_send, aa_recv, bb_send, bb_recv,
    c_send, c_recv, c_keep, s_send, s_recv, s_keep, o_send, o_recv, o_keep,
):
    core, y, x, z, tp = place()
    up, down = next_row(core, y), previous_row(core, y)
    ahead, behind = at(*up, x, z, tp), at(*down, x, z, tp)
    partner = at(core, y, x, z, 1 - tp)
    twin = at(1 - core, y, x, z, tp)
    side_core = core * (1 - x) + up[0] * x
    side_y = y * (1 - x) + up[1] * x
    side = at(side_core, side_y, 1 - x, z, tp)
    feed_core = core * x + down[0] * (1 - x)
    feed_y = y * x + down[1] * (1 - x)
    feed = at(feed_core, feed_y, 1 - x, z, tp)
    first_row = (core + y) == 0
    row = core * 4 + y
    peers = [at(core, y, x, lax.rem(z + d, 4), tp) for d in (1, 2, 3)]

    barrier = pltpu.get_barrier_semaphore()
    for other in [partner, twin, ahead, behind, side, feed, *peers]:
        pl.semaphore_signal(barrier, inc=1, device_id=other, device_id_type=MESH)

    def sink_target(n):
        slot = lax.rem(row * 2 + x + n, 16)
        return at(slot // 8, lax.rem(slot // 2, 4), lax.rem(slot, 2), z, tp)

    @pl.when(first_row)
    def _():
        for n in range(1, 16):
            pl.semaphore_signal(barrier, inc=1, device_id=sink_target(n), device_id_type=MESH)
        pl.semaphore_wait(barrier, 24)

    @pl.when(jnp.logical_not(first_row))
    def _():
        for x_home in (0, 1):
            pl.semaphore_signal(
                barrier, inc=1, device_id=at(0, 0, x_home, z, tp), device_id_type=MESH
            )
        pl.semaphore_wait(barrier, 11)

    size = 256 // CHUNKS
    spans = [pl.ds(c * size, size) for c in range(CHUNKS)]
    x_copies = [
        remote(x_hbm.at[:, s], x_far.at[:, s], x_send.at[c], x_recv.at[c], partner)
        for c, s in enumerate(spans)
    ]
    for copy in x_copies:
        copy.start()
    load_x = pltpu.make_async_copy(x_hbm, x_own, load_sem.at[0])
    load_kv = pltpu.make_async_copy(wkv_hbm, wkv_raw, load_sem.at[1])
    load_q = pltpu.make_async_copy(wq_hbm, wq_raw, load_sem.at[2])
    load_kv.start()
    load_q.start()
    load_x.start()
    load_kv.wait()

    @pl.loop(0, 4)
    def _(block):
        rows = pl.ds(pl.multiple_of(block * 512, 512), 512)
        spread[...] = wkv_raw[rows].reshape(4096, 128).astype(jnp.float32)
        kept = pl.ds(pl.multiple_of(block * 1024, 1024), 1024)
        for g in range(2):
            for c in range(2):
                at_column = (g * 2 + c) * 128
                wkv[kept, at_column:at_column + 128] = spread[
                    pl.ds(c * 2 + g, 1024, stride=4), :
                ].astype(jnp.bfloat16)

    load_q.wait()

    @pl.loop(0, 8)
    def _(block):
        rows = pl.ds(pl.multiple_of(block * 512, 512), 512)
        spread[...] = wq_raw[rows].reshape(4096, 128).astype(jnp.float32)
        for h in range(8):
            wq[rows, h * 128:(h + 1) * 128] = spread[pl.ds(h, 512, stride=8), :].astype(
                jnp.bfloat16
            )

    load_x.wait()
    own_rows = pl.ds(pl.multiple_of(tp * 2048, 2048), 2048)
    far_rows = pl.ds(pl.multiple_of((1 - tp) * 2048, 2048), 2048)

    def columns(n):
        return pl.ds(pl.multiple_of(n * 256, 256), 256)

    @pl.loop(0, 2)
    def _(n):
        acc_kv[:, :, columns(n)] = jnp.dot(
            x_own[...].reshape(512, 2048),
            wkv[own_rows, columns(n)],
            preferred_element_type=jnp.float32,
        ).reshape(2, 256, 256)

    @pl.loop(0, 4)
    def _(n):
        acc_q[:, :, columns(n)] = jnp.dot(
            x_own[...].reshape(512, 2048),
            wq[own_rows, columns(n)],
            preferred_element_type=jnp.float32,
        ).reshape(2, 256, 256)

    slab_start = (core * 32 + y * 8 + x * 4 + z) * 256
    pending = []
    kv_copies, q_copies, keeps, a_copies, b_copies, aa_copies, bb_copies = [], [], [], [], [], [], []

    def pass_on(c):
        s = spans[c]
        a_copies[c].wait_recv()
        aa = remote(
            kv_all.at[8:12, s], kv_all.at[0:4, s], aa_send.at[c], aa_recv.at[c], ahead
        )
        aa.start()
        aa_copies.append(aa)
        b_copies[c].wait_recv()
        bb = remote(
            kv_all.at[12:16, s], kv_all.at[4:8, s], bb_send.at[c], bb_recv.at[c], ahead
        )
        bb.start()
        bb_copies.append(bb)

    for c in range(CHUNKS):
        s = spans[c]
        x_copies[c].wait_recv()
        cosine, sine = cos_ref[s, :], sin_ref[s, :]

        @pl.loop(0, 2)
        def _(n):
            total = jnp.dot(
                x_far[:, s].reshape(2 * size, 2048),
                wkv[far_rows, columns(n)],
                preferred_element_type=jnp.float32,
            )
            for r in range(2):
                block = total[r * size:(r + 1) * size] + acc_kv[r, s, columns(n)]
                keys = turned(block[:, :128], cosine, sine).astype(jnp.bfloat16)
                both = jnp.concatenate([keys, block[:, 128:].astype(jnp.bfloat16)], axis=1)
                kv_stage[r * 2 + n, s, :] = both
                position = (
                    slab_start + c * size + lax.broadcasted_iota(jnp.int32, (size, 256), 0)
                )
                cache_stage[r, n, s, :] = jnp.where(
                    position < lens[r], both.astype(jnp.float32), 0.0
                ).astype(jnp.bfloat16)

        for d in (1, 2, 3):
            target = lax.rem(z + d, 4)
            copy = remote(
                kv_stage.at[target, s], kv_all.at[16 + z, s],
                kv_send.at[c, d - 1], kv_recv.at[c, d - 1], peers[d - 1],
            )
            copy.start()
            kv_copies.append(copy)
        keep = pltpu.make_async_copy(kv_stage.at[z, s], kv_all.at[16 + z, s], kv_keep.at[c])
        keep.start()

        @pl.loop(0, 4)
        def _(n):
            total = jnp.dot(
                x_far[:, s].reshape(2 * size, 2048),
                wq[far_rows, columns(n)],
                preferred_element_type=jnp.float32,
            )
            for r in range(2):
                block = total[r * size:(r + 1) * size] + acc_q[r, s, columns(n)]
                for k in range(2):
                    head = turned(block[:, k * 128:(k + 1) * 128], cosine, sine)
                    q_stage[r * 2 + n // 2, lax.rem(n, 2) * 2 + k, s, :] = head.astype(
                        jnp.bfloat16
                    )

        for d in (1, 2, 3):
            target = lax.rem(z + d, 4)
            copy = remote(
                q_stage.at[target, :, s], q_all.at[z, :, s],
                q_send.at[c, d - 1], q_recv.at[c, d - 1], peers[d - 1],
            )
            copy.start()
            q_copies.append(copy)
        q_own = pltpu.make_async_copy(q_stage.at[z, :, s], q_all.at[z, :, s], q_keep.at[c])
        q_own.start()
        keeps.append(q_own)

        keep.wait()
        for d in range(3):
            kv_copies[c * 3 + d].wait_recv()
        a = remote(kv_all.at[16:20, s], kv_all.at[8:12, s], a_send.at[c], a_recv.at[c], ahead)
        b = remote(kv_all.at[16:20, s], kv_all.at[12:16, s], b_send.at[c], b_recv.at[c], side)
        a.start()
        b.start()
        a_copies.append(a)
        b_copies.append(b)
        if c >= 1:
            pass_on(c - 1)

    cache_copy = remote(
        cache_stage.at[:, 1 - core], cache_out.at[:, core], c_send.at[0], c_recv.at[0], twin
    )
    cache_copy.start()
    cache_keep = pltpu.make_async_copy(
        cache_stage.at[:, core], cache_out.at[:, core], c_keep.at[0]
    )
    cache_keep.start()

    sink_sends = [
        remote(
            sink_stage, sink_all.at[x], s_send.at[n - 1], s_recv.at[x], sink_target(n)
        )
        for n in range(1, 16)
    ]
    sink_keep = pltpu.make_async_copy(sink_stage, sink_all.at[x], s_keep.at[0])

    @pl.when(first_row)
    def _():
        sink_stage[...] = jnp.dot(
            hot_ref[...], kv_all[16:20].reshape(1024, 256), preferred_element_type=jnp.float32
        ).astype(jnp.bfloat16)
        for copy in sink_sends:
            copy.start()
        sink_keep.start()

    for copy in keeps:
        copy.wait()
    for copy in q_copies:
        copy.wait_recv()
    group = row * 2 + x
    request = z // 2
    length = lens[request]
    key_at = lax.broadcasted_iota(jnp.int32, (256, 256), 0)
    query_at = lax.broadcasted_iota(jnp.int32, (256, 256), 1)

    def turn_values(first, count):
        @pl.loop(first, first + count)
        def _(slab):
            values[slab, :128, :] = (
                kv_all[slab, :, 128:].astype(jnp.float32).T.astype(jnp.bfloat16)
            )
            values[slab, 128:, :] = jnp.ones((16, 256), jnp.bfloat16)

    def rescale(j, h, new, gained):
        factor = jnp.exp2((peak[j, h] - new) * SCALE)
        peak[j, h] = new
        total[j, h] = (total[j, h].reshape(18, 8, 256) * factor[None]).reshape(144, 256) + gained

    def top_of(block):
        return jnp.broadcast_to(jnp.max(block, axis=0, keepdims=True), (8, 256))

    def fold(j, items):
        tops = []
        for h in range(4):
            top = peak[j, h]
            for i, (slab, visible) in enumerate(items):
                block = lax.dot_general(
                    kv_all[slab, :, :128], q_all[j, h], (((1,), (1,)), ((), ())),
                    preferred_element_type=jnp.float32,
                )
                if visible is not None:
                    block = jnp.where(visible, block, NEG_FILL)
                scores[h, i] = block
                top = jnp.maximum(top, jnp.max(block.reshape(32, 8, 256), axis=0))
            tops.append(top_of(top))
        for h in range(4):
            shift = tops[h] * SCALE
            gained = None
            for i, (slab, _) in enumerate(items):
                weights = jnp.exp2(
                    (scores[h, i] * SCALE).reshape(32, 8, 256) - shift[None]
                ).reshape(256, 256)
                part = jnp.dot(
                    values[slab], weights.astype(jnp.bfloat16),
                    preferred_element_type=jnp.float32,
                )
                gained = part if gained is None else gained + part
            rescale(j, h, tops[h], gained)

    turn_values(16, 4)

    @pl.loop(0, 4)
    def _(j):
        for h in range(4):
            peak[j, h] = jnp.full((8, 256), NEG_FILL, jnp.float32)
            total[j, h] = jnp.zeros((144, 256), jnp.float32)
        fold(j, [(16 + j, key_at <= query_at)])

    pass_on(CHUNKS - 1)
    turn_values(8, 8)

    for back in (1, 2):
        @pl.when(group >= back)
        def _():
            @pl.loop(0, 4)
            def _(j):
                fold(j, [(20 - 4 * back - 4 + i, None) for i in range(4)])

    for copy in aa_copies + bb_copies:
        copy.wait_recv()
    turn_values(0, 8)
    @pl.when(first_row)
    def _():
        sink_keep.wait()
        for copy in sink_sends:
            copy.wait_send()
        remote(sink_stage, sink_all.at[1 - x], s_send.at[0], s_recv.at[1 - x], partner).wait_recv()

    @pl.when(jnp.logical_not(first_row))
    def _():
        for home in (0, 1):
            remote(
                sink_stage, sink_all.at[home], s_send.at[0], s_recv.at[home], partner
            ).wait_recv()
    sink_kv = (sink_all[0].astype(jnp.float32) + sink_all[1].astype(jnp.float32)).astype(
        jnp.bfloat16
    )
    sink_values[:128, :] = (
        jnp.concatenate(
            [sink_kv[:, 128:].astype(jnp.float32), jnp.zeros((112, 128), jnp.float32)], axis=0
        ).T.astype(jnp.bfloat16)
    )
    sink_values[128:, :] = jnp.ones((16, 128), jnp.bfloat16)
    out_columns = pl.ds(pl.multiple_of(lax.rem(z, 2) * 512, 512), 512)

    @pl.loop(0, 4)
    def _(turn):
        j = lax.rem(z + 1 + turn, 4)

        @pl.when(group >= 3)
        def _():
            fold(j, [(4 + i, None) for i in range(4)])

        @pl.when(group >= 4)
        def _():
            edges = [(jnp.where(t < j, 16 + t, t + 1), None) for t in range(3)]
            fold(j, edges + [(j, key_at > query_at)])

        @pl.when(group < 4)
        def _():
            def inner(t, carry):
                fold(j, [(16 + t, None)])
                return carry

            lax.fori_loop(0, j, inner, 0)

        first = (group * 4 + j) * 256
        far = first + query_at[:16] - sink_pos[...] >= WINDOW
        for h in range(4):
            block = lax.dot_general(
                sink_kv[:, :128], q_all[j, h], (((1,), (1,)), ((), ())),
                preferred_element_type=jnp.float32,
            )
            block = jnp.where(far, block, NEG_FILL)
            top = top_of(
                jnp.maximum(peak[j, h], jnp.max(block.reshape(2, 8, 256), axis=0))
            )
            weights = jnp.exp2((block * SCALE).reshape(2, 8, 256) - (top * SCALE)[None])
            weights = jnp.concatenate(
                [weights.reshape(16, 256), jnp.zeros((112, 256), jnp.float32)], axis=0
            )
            rescale(
                j, h, top,
                jnp.dot(
                    sink_values[...], weights.astype(jnp.bfloat16),
                    preferred_element_type=jnp.float32,
                ),
            )
            mixed = (total[j, h, :128] / total[j, h, 128:129]).T
            live = first + lax.broadcasted_iota(jnp.int32, (256, 128), 0) < length
            stage[turn, :, h * 128:(h + 1) * 128] = jnp.where(live, mixed, 0.0).astype(
                jnp.bfloat16
            )

        home = out_ref.at[request, :, out_columns]

        @pl.when(turn < 3)
        def _():
            remote(
                stage.at[turn], home, o_send.at[turn], o_recv.at[turn],
                at(core, y, x, j, tp),
            ).start()

        @pl.when(turn == 3)
        def _():
            pltpu.make_async_copy(stage.at[turn], home, o_keep.at[0]).start()

    pltpu.make_async_copy(
        stage.at[3], out_ref.at[request, :, out_columns], o_keep.at[0]
    ).wait()
    for turn in range(3):
        source = lax.rem(z + 3 - turn, 4)
        landed = out_ref.at[
            source // 2, :, pl.ds(pl.multiple_of(lax.rem(source, 2) * 512, 512), 512)
        ]
        remote(
            stage.at[turn], landed, o_send.at[turn], o_recv.at[turn], peers[turn]
        ).wait()
    cache_keep.wait()
    cache_copy.wait()
    for copy in aa_copies + bb_copies + q_copies + kv_copies + a_copies + b_copies + x_copies:
        copy.wait_send()


def dma(*shape):
    return pltpu.SemaphoreType.DMA(shape)


def per_device(prompt_states, q_weight, kv_weight, lengths, sink_positions):
    bf16 = jnp.bfloat16
    core, y, x, z, tp = place()
    group = (core * 4 + y) * 2 + x
    kv_rows = kv_weight.reshape(2048, 8, 128)
    positions = (group * 4 + z) * 256 + jnp.arange(256, dtype=jnp.int32)
    ladder = jnp.arange(64, dtype=jnp.float32) * (2.0 / 128)
    inv_freq = jnp.exp(-math.log(ROPE_BASE) * ladder)
    angles = positions.astype(jnp.float32)[:, None] * inv_freq[None, :]
    cosine, sine = jnp.cos(angles), jnp.sin(angles)
    cos_table = jnp.concatenate([cosine, cosine], axis=1)
    sin_table = jnp.concatenate([-sine, sine], axis=1)
    sinks = jnp.where(z < 2, sink_positions[0], sink_positions[1])
    group_pos = group * 1024 + jnp.arange(1024, dtype=jnp.int32)
    hot = (sinks[:, None] == group_pos[None, :]).astype(bf16)
    hot = jnp.pad(hot, ((0, 12), (0, 0)))
    earlier = jnp.arange(4)[None, :] < jnp.arange(4)[:, None]
    repeated = jnp.any((sinks[:, None] == sinks[None, :]) & earlier, axis=1)
    sink_column = jnp.pad(jnp.where(repeated, FAR, sinks), (0, 12), constant_values=FAR)
    sink_column = jnp.broadcast_to(sink_column[:, None], (16, 256))

    anyspace = pl.BlockSpec(memory_space=pl.ANY)
    vmem = pl.BlockSpec(memory_space=pltpu.VMEM)
    smem = pl.BlockSpec(memory_space=pltpu.SMEM)
    shape = jax.ShapeDtypeStruct
    f32 = jnp.float32
    attended, cache = pl.pallas_call(
        layer_kernel,
        out_shape=(shape((2, 256, 1024), bf16), shape((2, 2, 256, 256), bf16)),
        in_specs=[smem, anyspace, anyspace, anyspace, vmem, vmem, vmem, vmem],
        out_specs=(anyspace, anyspace),
        scratch_shapes=[
            pltpu.VMEM((2, 256, 2048), bf16),
            pltpu.VMEM((2, 256, 2048), bf16),
            pltpu.VMEM((4096, 8, 128), bf16),
            pltpu.VMEM((2048, 8, 128), bf16),
            pltpu.VMEM((4096, 128), f32),
            pltpu.VMEM((4096, 1024), bf16),
            pltpu.VMEM((4096, 512), bf16),
            pltpu.VMEM((2, 256, 1024), f32),
            pltpu.VMEM((2, 256, 512), f32),
            pltpu.VMEM((4, 4, 256, 128), bf16),
            pltpu.VMEM((4, 256, 256), bf16),
            pltpu.VMEM((2, 2, 256, 256), bf16),
            pltpu.VMEM((4, 4, 256, 128), bf16),
            pltpu.VMEM((20, 256, 256), bf16),
            pltpu.VMEM((2, 16, 256), bf16),
            pltpu.VMEM((16, 256), bf16),
            pltpu.VMEM((20, 144, 256), bf16),
            pltpu.VMEM((144, 128), bf16),
            pltpu.VMEM((4, 4, 8, 256), f32),
            pltpu.VMEM((4, 4, 144, 256), f32),
            pltpu.VMEM((4, 4, 256, 256), f32),
            pltpu.VMEM((4, 256, 512), bf16),
            dma(CHUNKS), dma(CHUNKS), dma(3),
            dma(CHUNKS, 3), dma(CHUNKS, 3), dma(CHUNKS),
            dma(CHUNKS, 3), dma(CHUNKS, 3), dma(CHUNKS),
            dma(CHUNKS), dma(CHUNKS), dma(CHUNKS), dma(CHUNKS),
            dma(CHUNKS), dma(CHUNKS), dma(CHUNKS), dma(CHUNKS),
            dma(1), dma(1), dma(1), dma(15), dma(2), dma(1),
            dma(3), dma(3), dma(1),
        ],
        compiler_params=pltpu.CompilerParams(
            collective_id=0, has_side_effects=True, vmem_limit_bytes=VMEM_BYTES
        ),
    )(lengths, prompt_states, q_weight, kv_rows, cos_table, sin_table, hot, sink_column)
    return attended, cache.reshape(2, 1, 2, 1, 256, 256)


def solution(mesh):
    placed = (
        P(None, ("grp", "seq"), "tp"),
        P(None, "tp", None),
        P(None, None, "tp", None),
        P(),
        P(),
    )
    return jax.shard_map(
        per_device,
        mesh=mesh,
        in_specs=placed,
        out_specs=(P(None, ("grp", "seq"), "tp"), P(None, ("tp", "grp"), None, "seq", None, None)),
        check_vma=False,
    )
```

time: 192 us -> 121 us (0.63)
  Pallas kernels: 157 us -> 111 us
  local copies, waits for them, and re-layouts: 30.3 us -> 4.8 us
    pallas_call x2 -> x1, Pallas kernels: 157 us -> 111 us  [per_device(): pl.pallas_call(layer_kernel, out_shape=(shape((2, 256, 1024), bf16), shap...]
    transpose x1 -> x0, local copies, waits for them, and re-layouts: 10.8 us -> none  [per_device(): wkv = jnp.transpose(kv_weight, (0, 2, 1, 3)).reshape(4096, 512)]
    unnamed x5 -> x2, local copies, waits for them, and re-layouts: 11.8 us -> 4.13 us
    reshape x1 -> x0, local copies, waits for them, and re-layouts: 7.21 us -> none  [per_device(): wkv = jnp.transpose(kv_weight, (0, 2, 1, 3)).reshape(4096, 512)]
where the time goes in v1:
time: 121 us; the launch traced here: 120 us
  Pallas kernels  111 us (92%)
  local copies, waits for them, and re-layouts  4.8 us (4%)
  other arithmetic  3.79 us (3%)
    pallas_call x1, Pallas kernels, per_device(): pl.pallas_call(layer_kernel, out_shape=(shape((2, 256, 1024), bf16), shap...  111 us
    unnamed x2, local copies, waits for them, and re-layouts  4.13 us

profile of v1, /device:TPU:1, one launch (start us, length us, event | category | flops | bytes accessed | tf_op | source)
XLA Modules:
  0.0 120.3 jit_solution(4207962055359114189)
XLA Ops:
  0.7 0.8 fusion.3
  1.4 0.2 fusion.2
  1.6 0.8 broadcast_select_fusion.1
  2.4 0.1 broadcast_compare_fusion
  2.5 0.7 broadcast_in_dim.6.sink_pos
  3.2 0.6 pad_convert_fusion.hot_ref
  3.8 0.5 fusion
  4.3 0.8 pad_maximum_fusion
  5.2 111.0 %shard_map.68 = (bf16[2,256,1024]{2,1,0:T(8,128)(2,1)}, bf16[2,2,256,256]{3,2,1,0:T(8,128)(2,1)}) custom-call(s32[2]{0:T(128)} %lens.1, bf16[2,256,2048]{2,1,0:T(8,128)(2,1)} %x_hbm.1, bf16[4096,8,128]{2,1,0:T(8,128)(2,1)} %wq_hbm.1, bf16[2048,8,128]{2,1,0:T(8,128)(2,1)} %bitcast.8, f32[256,128]{1,0:T(8,128)} %get-tuple-element.13.cos_ref, ...), custom_call_target="tpu_custom_call" | custom-call | tf_op jit(solution)/shard_map/pallas_call | solution.py:492
  116.2 2.3 %copy.11 = bf16[2,256,1024]{2,1,0:T(8,128)(2,1)} copy(bf16[2,256,1024]{2,1,0:T(8,128)(2,1)} %get-tuple-element.17) | data formatting | bytes 2097152
  118.5 1.9 %copy.12 = bf16[2,1,2,1,256,256]{5,4,3,2,1,0:T(8,128)(2,1)} copy(bf16[2,1,2,1,256,256]{5,4,3,2,1,0:T(8,128)(2,1)} %bitcast.9) | data formatting | bytes 1048576
  (4 shorter events, 0.0 us)

commit v2 on v1

--- a/solution.py
+++ b/solution.py
@@ -13,6 +13,7 @@
 FAR = 1 << 30
 MESH = pl.DeviceIdType.MESH
 CHUNKS = 4
+EARLY_SIDE = 2
 VMEM_BYTES = 60 * 2**20
 
 
@@ -54,7 +55,7 @@
 
 
 def layer_kernel(
-    lens, x_hbm, wq_hbm, wkv_hbm, cos_ref, sin_ref, hot_ref, sink_pos,
+    lens, sinks, x_hbm, wq_hbm, wkv_hbm, cos_ref, sin_ref,
     out_ref, cache_out,
     x_own, x_far, wq_raw, wkv_raw, spread, wq, wkv, acc_q, acc_kv, q_stage, kv_stage, cache_stage,
     q_all, kv_all, sink_all, sink_stage, values, sink_values, peak, total, scores, stage,
@@ -67,18 +68,15 @@
     ahead, behind = at(*up, x, z, tp), at(*down, x, z, tp)
     partner = at(core, y, x, z, 1 - tp)
     twin = at(1 - core, y, x, z, tp)
-    side_core = core * (1 - x) + up[0] * x
-    side_y = y * (1 - x) + up[1] * x
-    side = at(side_core, side_y, 1 - x, z, tp)
-    feed_core = core * x + down[0] * (1 - x)
-    feed_y = y * x + down[1] * (1 - x)
-    feed = at(feed_core, feed_y, 1 - x, z, tp)
+    side = at(core, y, 1 - x, z, tp)
+    beyond = at(lax.rem(core + (y + 2) // 4, 2), lax.rem(y + 2, 4), x, z, tp)
+    before = at(lax.rem(core + (5 - y) // 4, 2), lax.rem(y + 2, 4), x, z, tp)
     first_row = (core + y) == 0
     row = core * 4 + y
     peers = [at(core, y, x, lax.rem(z + d, 4), tp) for d in (1, 2, 3)]
 
     barrier = pltpu.get_barrier_semaphore()
-    for other in [partner, twin, ahead, behind, side, feed, *peers]:
+    for other in [partner, twin, ahead, behind, beyond, before, side, *peers]:
         pl.semaphore_signal(barrier, inc=1, device_id=other, device_id_type=MESH)
 
     def sink_target(n):
@@ -89,7 +87,7 @@
     def _():
         for n in range(1, 16):
             pl.semaphore_signal(barrier, inc=1, device_id=sink_target(n), device_id_type=MESH)
-        pl.semaphore_wait(barrier, 24)
+        pl.semaphore_wait(barrier, 25)
 
     @pl.when(jnp.logical_not(first_row))
     def _():
@@ -97,8 +95,16 @@
             pl.semaphore_signal(
                 barrier, inc=1, device_id=at(0, 0, x_home, z, tp), device_id_type=MESH
             )
-        pl.semaphore_wait(barrier, 11)
-
+        pl.semaphore_wait(barrier, 12)
+
+    request = z // 2
+    marks = [sinks[request, n] for n in range(4)]
+    fresh = []
+    for n in range(4):
+        mark = marks[n]
+        for earlier in marks[:n]:
+            mark = jnp.where(marks[n] == earlier, FAR, mark)
+        fresh.append(mark)
     size = 256 // CHUNKS
     spans = [pl.ds(c * size, size) for c in range(CHUNKS)]
     x_copies = [
@@ -163,26 +169,37 @@
 
     slab_start = (core * 32 + y * 8 + x * 4 + z) * 256
     pending = []
-    kv_copies, q_copies, keeps, a_copies, b_copies, aa_copies, bb_copies = [], [], [], [], [], [], []
-
-    def pass_on(c):
+    kv_copies, q_copies, keeps, a_copies, b_copies, aa_copies = [], [], [], [], [], []
+
+    side_source = pl.ds(16 - 8 * x, 4)
+
+    def to_side(c):
         s = spans[c]
         a_copies[c].wait_recv()
-        aa = remote(
-            kv_all.at[8:12, s], kv_all.at[0:4, s], aa_send.at[c], aa_recv.at[c], ahead
+        b = remote(
+            kv_all.at[side_source, s], kv_all.at[12:16, s], b_send.at[c], b_recv.at[c], side
         )
-        aa.start()
-        aa_copies.append(aa)
-        b_copies[c].wait_recv()
-        bb = remote(
+        b.start()
+        b_copies.append(b)
+
+    def from_side(c):
+        s = pl.ds(pl.multiple_of(c * size, size), size)
+        remote(
+            kv_all.at[side_source, s], kv_all.at[12:16, s], b_send.at[c], b_recv.at[c], side
+        ).wait_recv()
+        remote(
             kv_all.at[12:16, s], kv_all.at[4:8, s], bb_send.at[c], bb_recv.at[c], ahead
-        )
-        bb.start()
-        bb_copies.append(bb)
+        ).start()
 
     for c in range(CHUNKS):
         s = spans[c]
         x_copies[c].wait_recv()
+        if c == 2:
+            for early in range(EARLY_SIDE):
+                to_side(early)
+        if c == CHUNKS - 1:
+            for late in range(EARLY_SIDE, CHUNKS - 1):
+                to_side(late)
         cosine, sine = cos_ref[s, :], sin_ref[s, :]
 
         @pl.loop(0, 2)
@@ -246,13 +263,14 @@
         for d in range(3):
             kv_copies[c * 3 + d].wait_recv()
         a = remote(kv_all.at[16:20, s], kv_all.at[8:12, s], a_send.at[c], a_recv.at[c], ahead)
-        b = remote(kv_all.at[16:20, s], kv_all.at[12:16, s], b_send.at[c], b_recv.at[c], side)
         a.start()
-        b.start()
         a_copies.append(a)
-        b_copies.append(b)
-        if c >= 1:
-            pass_on(c - 1)
+        aa = remote(kv_all.at[16:20, s], kv_all.at[0:4, s], aa_send.at[c], aa_recv.at[c], beyond)
+        aa.start()
+        aa_copies.append(aa)
+        if c == CHUNKS - 1:
+            for early in range(EARLY_SIDE):
+                from_side(early)
 
     cache_copy = remote(
         cache_stage.at[:, 1 - core], cache_out.at[:, core], c_send.at[0], c_recv.at[0], twin
@@ -273,8 +291,14 @@
 
     @pl.when(first_row)
     def _():
+        mark_row = lax.broadcasted_iota(jnp.int32, (16, 1024), 0)
+        token = row * 2048 + x * 1024 + lax.broadcasted_iota(jnp.int32, (16, 1024), 1)
+        wanted = jnp.full((16, 1024), FAR, jnp.int32)
+        for n in range(4):
+            wanted = jnp.where(mark_row == n, marks[n], wanted)
+        hot = jnp.where(token == wanted, 1.0, 0.0).astype(jnp.bfloat16)
         sink_stage[...] = jnp.dot(
-            hot_ref[...], kv_all[16:20].reshape(1024, 256), preferred_element_type=jnp.float32
+            hot, kv_all[16:20].reshape(1024, 256), preferred_element_type=jnp.float32
         ).astype(jnp.bfloat16)
         for copy in sink_sends:
             copy.start()
@@ -285,7 +309,6 @@
     for copy in q_copies:
         copy.wait_recv()
     group = row * 2 + x
-    request = z // 2
     length = lens[request]
     key_at = lax.broadcasted_iota(jnp.int32, (256, 256), 0)
     query_at = lax.broadcasted_iota(jnp.int32, (256, 256), 1)
@@ -343,19 +366,53 @@
             total[j, h] = jnp.zeros((144, 256), jnp.float32)
         fold(j, [(16 + j, key_at <= query_at)])
 
-    pass_on(CHUNKS - 1)
-    turn_values(8, 8)
-
-    for back in (1, 2):
-        @pl.when(group >= back)
+    to_side(CHUNKS - 1)
+    turn_values(8, 4)
+
+    @pl.when(group >= 2)
+    def _():
+        @pl.loop(0, 4)
+        def _(j):
+            fold(j, [(8 + i, None) for i in range(4)])
+
+    for copy in aa_copies:
+        copy.wait_recv()
+    turn_values(0, 4)
+
+    @pl.loop(0, CHUNKS)
+    def _(j):
+        @pl.when(j < CHUNKS - EARLY_SIDE)
         def _():
-            @pl.loop(0, 4)
-            def _(j):
-                fold(j, [(20 - 4 * back - 4 + i, None) for i in range(4)])
-
-    for copy in aa_copies + bb_copies:
+            from_side(j + EARLY_SIDE)
+
+        @pl.when(group >= 4)
+        def _():
+            edges = [(jnp.where(t < j, 16 + t, t + 1), None) for t in range(3)]
+            fold(j, edges + [(j, key_at > query_at)])
+
+        @pl.when(group < 4)
+        def _():
+            def inner(t, carry):
+                fold(j, [(16 + t, None)])
+                return carry
+
+            lax.fori_loop(0, j, inner, 0)
+
+    turn_values(12, 4)
+
+    @pl.when(group >= 1)
+    def _():
+        @pl.loop(0, 4)
+        def _(j):
+            fold(j, [(12 + i, None) for i in range(4)])
+
+    bb_copies = [
+        remote(kv_all.at[12:16, s], kv_all.at[4:8, s], bb_send.at[c], bb_recv.at[c], ahead)
+        for c, s in enumerate(spans)
+    ]
+    for copy in bb_copies:
         copy.wait_recv()
-    turn_values(0, 8)
+    turn_values(4, 4)
     @pl.when(first_row)
     def _():
         sink_keep.wait()
@@ -378,6 +435,10 @@
         ).T.astype(jnp.bfloat16)
     )
     sink_values[128:, :] = jnp.ones((16, 128), jnp.bfloat16)
+    mark_at = lax.broadcasted_iota(jnp.int32, (16, 256), 0)
+    sink_at = jnp.full((16, 256), FAR, jnp.int32)
+    for n in range(4):
+        sink_at = jnp.where(mark_at == n, fresh[n], sink_at)
     out_columns = pl.ds(pl.multiple_of(lax.rem(z, 2) * 512, 512), 512)
 
     @pl.loop(0, 4)
@@ -388,21 +449,8 @@
         def _():
             fold(j, [(4 + i, None) for i in range(4)])
 
-        @pl.when(group >= 4)
-        def _():
-            edges = [(jnp.where(t < j, 16 + t, t + 1), None) for t in range(3)]
-            fold(j, edges + [(j, key_at > query_at)])
-
-        @pl.when(group < 4)
-        def _():
-            def inner(t, carry):
-                fold(j, [(16 + t, None)])
-                return carry
-
-            lax.fori_loop(0, j, inner, 0)
-
         first = (group * 4 + j) * 256
-        far = first + query_at[:16] - sink_pos[...] >= WINDOW
+        far = first + query_at[:16] - sink_at >= WINDOW
         for h in range(4):
             block = lax.dot_general(
                 sink_kv[:, :128], q_all[j, h], (((1,), (1,)), ((), ())),
@@ -475,15 +523,6 @@
     cosine, sine = jnp.cos(angles), jnp.sin(angles)
     cos_table = jnp.concatenate([cosine, cosine], axis=1)
     sin_table = jnp.concatenate([-sine, sine], axis=1)
-    sinks = jnp.where(z < 2, sink_positions[0], sink_positions[1])
-    group_pos = group * 1024 + jnp.arange(1024, dtype=jnp.int32)
-    hot = (sinks[:, None] == group_pos[None, :]).astype(bf16)
-    hot = jnp.pad(hot, ((0, 12), (0, 0)))
-    earlier = jnp.arange(4)[None, :] < jnp.arange(4)[:, None]
-    repeated = jnp.any((sinks[:, None] == sinks[None, :]) & earlier, axis=1)
-    sink_column = jnp.pad(jnp.where(repeated, FAR, sinks), (0, 12), constant_values=FAR)
-    sink_column = jnp.broadcast_to(sink_column[:, None], (16, 256))
-
     anyspace = pl.BlockSpec(memory_space=pl.ANY)
     vmem = pl.BlockSpec(memory_space=pltpu.VMEM)
     smem = pl.BlockSpec(memory_space=pltpu.SMEM)
@@ -492,7 +531,7 @@
     attended, cache = pl.pallas_call(
         layer_kernel,
         out_shape=(shape((2, 256, 1024), bf16), shape((2, 2, 256, 256), bf16)),
-        in_specs=[smem, anyspace, anyspace, anyspace, vmem, vmem, vmem, vmem],
+        in_specs=[smem, smem, anyspace, anyspace, anyspace, vmem, vmem],
         out_specs=(anyspace, anyspace),
         scratch_shapes=[
             pltpu.VMEM((2, 256, 2048), bf16),
@@ -528,7 +567,7 @@
         compiler_params=pltpu.CompilerParams(
             collective_id=0, has_side_effects=True, vmem_limit_bytes=VMEM_BYTES
         ),
-    )(lengths, prompt_states, q_weight, kv_rows, cos_table, sin_table, hot, sink_column)
+    )(lengths, sink_positions, prompt_states, q_weight, kv_rows, cos_table, sin_table)
     return attended, cache.reshape(2, 1, 2, 1, 256, 256)
 
 

time: 121 us -> 106 us (0.88); the launches traced: 120 us -> 104 us
  Pallas kernels: 111 us -> 97.8 us
  other arithmetic: 3.79 us -> 1.39 us
    pallas_call x1, Pallas kernels: 111 us -> 97.8 us  [per_device(): pl.pallas_call(layer_kernel, out_shape=(shape((2, 256, 1024), bf16), shap...]
    select_n x2 -> x0, other arithmetic: 1.52 us -> none  [the longest x1 0.76 us: per_device(): jnp.where(repeated, FAR, sinks)]
where the time goes in v2:
time: 106 us; the launch traced here: 104 us
  Pallas kernels  97.8 us (92%)
  local copies, waits for them, and re-layouts  4.13 us (4%)
  other arithmetic  1.39 us (1%)
    pallas_call x1, Pallas kernels, per_device(): pl.pallas_call(layer_kernel, out_shape=(shape((2, 256, 1024), bf16), shap...  97.8 us
    unnamed x2, local copies, waits for them, and re-layouts  4.13 us

profile of v2, /device:TPU:1, one launch (start us, length us, event | category | flops | bytes accessed | tf_op | source)
XLA Modules:
  0.0 104.0 jit_solution(3128912109259545500)
XLA Ops:
  0.7 0.5 fusion
  1.2 0.8 pad_maximum_fusion
  2.1 97.8 %shard_map.68 = (bf16[2,256,1024]{2,1,0:T(8,128)(2,1)}, bf16[2,2,256,256]{3,2,1,0:T(8,128)(2,1)}) custom-call(s32[2]{0:T(128)} %lens.1, s32[2,4]{1,0:T(2,128)} %sinks.1, bf16[2,256,2048]{2,1,0:T(8,128)(2,1)} %x_hbm.1, bf16[4096,8,128]{2,1,0:T(8,128)(2,1)} %wq_hbm.1, bf16[2048,8,128]{2,1,0:T(8,128)(2,1)} %bitcast.4, f32[256,128]{1,0:T(8,128)} %get-tuple-element.11.cos_ref, ...), custom_call_target="tpu_custom_call" | custom-call | tf_op jit(solution)/shard_map/pallas_call | solution.py:531
  99.9 2.3 %copy.10 = bf16[2,256,1024]{2,1,0:T(8,128)(2,1)} copy(bf16[2,256,1024]{2,1,0:T(8,128)(2,1)} %get-tuple-element.15) | data formatting | bytes 2097152
  102.2 1.9 %copy.11 = bf16[2,1,2,1,256,256]{5,4,3,2,1,0:T(8,128)(2,1)} copy(bf16[2,1,2,1,256,256]{5,4,3,2,1,0:T(8,128)(2,1)} %bitcast.5) | data formatting | bytes 1048576
  (2 shorter events, 0.0 us)

commit v3 on v2

--- a/solution.py
+++ b/solution.py
@@ -304,6 +304,7 @@
             copy.start()
         sink_keep.start()
 
+    to_side(CHUNKS - 1)
     for copy in keeps:
         copy.wait()
     for copy in q_copies:
@@ -366,7 +367,6 @@
             total[j, h] = jnp.zeros((144, 256), jnp.float32)
         fold(j, [(16 + j, key_at <= query_at)])
 
-    to_side(CHUNKS - 1)
     turn_values(8, 4)
 
     @pl.when(group >= 2)

time: 106 us -> 108 us (1.019)
  Pallas kernels: 97.8 us -> 101 us
    pallas_call x1, Pallas kernels: 97.8 us -> 101 us  [per_device(): pl.pallas_call(layer_kernel, out_shape=(shape((2, 256, 1024), bf16), shap...]
where the time goes in v3:
time: 108 us; the launch traced here: 107 us
  Pallas kernels  101 us (94%)
  local copies, waits for them, and re-layouts  4.13 us (4%)
  other arithmetic  1.39 us (1%)
    pallas_call x1, Pallas kernels, per_device(): pl.pallas_call(layer_kernel, out_shape=(shape((2, 256, 1024), bf16), shap...  101 us
    unnamed x2, local copies, waits for them, and re-layouts  4.13 us

profile of v3, /device:TPU:1, one launch (start us, length us, event | category | flops | bytes accessed | tf_op | source)
XLA Modules:
  0.0 106.8 jit_solution(14716386723191264616)
XLA Ops:
  0.7 0.5 fusion
  1.2 0.8 pad_maximum_fusion
  2.1 100.6 %shard_map.68 = (bf16[2,256,1024]{2,1,0:T(8,128)(2,1)}, bf16[2,2,256,256]{3,2,1,0:T(8,128)(2,1)}) custom-call(s32[2]{0:T(128)} %lens.1, s32[2,4]{1,0:T(2,128)} %sinks.1, bf16[2,256,2048]{2,1,0:T(8,128)(2,1)} %x_hbm.1, bf16[4096,8,128]{2,1,0:T(8,128)(2,1)} %wq_hbm.1, bf16[2048,8,128]{2,1,0:T(8,128)(2,1)} %bitcast.4, f32[256,128]{1,0:T(8,128)} %get-tuple-element.11.cos_ref, ...), custom_call_target="tpu_custom_call" | custom-call | tf_op jit(solution)/shard_map/pallas_call | solution.py:531
  102.6 2.3 %copy.10 = bf16[2,256,1024]{2,1,0:T(8,128)(2,1)} copy(bf16[2,256,1024]{2,1,0:T(8,128)(2,1)} %get-tuple-element.15) | data formatting | bytes 2097152
  104.9 1.9 %copy.11 = bf16[2,1,2,1,256,256]{5,4,3,2,1,0:T(8,128)(2,1)} copy(bf16[2,1,2,1,256,256]{5,4,3,2,1,0:T(8,128)(2,1)} %bitcast.5) | data formatting | bytes 1048576
  (2 shorter events, 0.0 us)
